TPU v7x, 512 devices: a whole 4x4x16 slice. The times are simulated.
512 devices in a mesh: dp: 32 (over y, x, core), tensor: 16 (over z).
Axes of the slice: x: 4, y: 4, z: 16, core: 2. Of those that a mesh axis runs over, the one named last changes fastest.
Arguments:
- tokens: bfloat16 [16384, 8192], P('dp', 'tensor'), may hold values from -6 to 6
- out_grad: bfloat16 [16384, 28672], P('dp', 'tensor'), may hold values from -6 to 6
- galore_basis: bfloat16 [8192, 512], P('tensor'), may hold values from -0.0625 to 0.0625
- first_moment: float32 [512, 28672], P('dp', 'tensor'), may hold values from -4 to 4
- second_moment: float32 [512, 28672], P('dp', 'tensor'), may hold values from 0.05 to 5
- list_lengths: int32 [128], P('dp'), may hold values from 1 to 128, as said below
Outputs:
- new_first: float32 [512, 28672], P('dp', 'tensor')
- new_second: float32 [512, 28672], P('dp', 'tensor')
- weight_step: bfloat16 [8192, 28672], P('dp', 'tensor')
Inputs may be any that keep to these rules, and one draw needn't show every extreme that they name: `list_lengths`: live slots of a list come first in its 128 slots.
All inputs are finite; a program needn't handle non-finite values.
Results may differ from a plain program's by a relative error of at most 0.0051.
Values may be sent and summed in bfloat16 or wider, within the bound.
No kernel may reach another device: no remote copies, remote signals or barrier semaphores. Data moves between devices by JAX's collectives and lax.ppermute only.
A program may use at most 64 MiB of HBM per device.

v0:
```python
import jax
import jax.numpy as jnp
from jax import lax
from jax.sharding import PartitionSpec as P

SLOTS = 128
STEP = 1000
beta_first = 0.9
beta_second = 0.999
epsilon = 1e-08
bf16 = jnp.bfloat16
f32 = jnp.float32


def exchange(tiles, axis, groups=None):
    return lax.all_to_all(
        tiles, axis, split_axis=0, concat_axis=0, tiled=True, axis_index_groups=groups
    )


def copies_to_all(x, axis, peers, groups=None):
    return exchange(jnp.broadcast_to(x, (peers, *x.shape)), axis, groups)


def token_weights(list_lengths):
    slot_index = jnp.arange(SLOTS, dtype=jnp.int32)
    live_slots = slot_index[None, :] < list_lengths[:, None]
    scaled = jnp.where(
        live_slots, 1.0 / list_lengths[:, None].astype(jnp.float32), jnp.float32(0.0)
    )
    return scaled.reshape(-1)


def basis_routes(chips, splits):
    return [
        ((2 * k + b) * splits + s, (2 * s + b) * splits + (k - s) % splits)
        for k in range(chips)
        for b in range(2)
        for s in range(splits)
    ]


def body(tokens, out_grad, galore_basis, first_moment, second_moment, list_lengths):
    replicas = lax.axis_size("dp")
    splits = lax.axis_size("tensor")
    chips = replicas // 2
    replica = lax.axis_index("dp")
    core = replica % 2
    rank = galore_basis.shape[1]
    owned = rank // replicas
    columns = out_grad.shape[1]
    slots = tokens.shape[0]
    same_core = [[2 * i + c for i in range(chips)] for c in range(2)]
    partner = [(i, i ^ 1) for i in range(replicas)]
    block_rows = galore_basis.shape[0] * splits // replicas
    half_block = lax.dynamic_slice_in_dim(galore_basis, core * block_rows, block_rows, 0)
    local_basis = lax.ppermute(half_block, ("dp", "tensor"), basis_routes(chips, splits))
    partial = lax.dot_general(
        galore_basis, tokens, (((0,), (1,)), ((), ())), preferred_element_type=f32
    ).astype(bf16)
    arrived = exchange(partial.reshape(splits, rank // splits, slots), "tensor")
    coordinates = arrived.astype(f32).sum(axis=0)
    weighted = (coordinates * token_weights(list_lengths)[None, :]).astype(bf16)
    weighted = lax.all_gather(weighted, "tensor", axis=0, tiled=True)
    by_owner = weighted.reshape(chips, 2, owned, slots)
    other = lax.dynamic_index_in_dim(by_owner, 1 - core, 1, keepdims=False).reshape(
        rank // 2, slots
    )
    own = lax.dynamic_index_in_dim(by_owner, core, 1, keepdims=False).reshape(rank // 2, slots)
    sent = jnp.dot(other, out_grad, preferred_element_type=f32).astype(bf16)
    received = lax.ppermute(sent, "dp", partner)
    kept = jnp.dot(own, out_grad, preferred_element_type=f32)
    chip_sum = (kept + received.astype(f32)).astype(bf16).reshape(chips, owned, columns)
    gradient = exchange(chip_sum, "dp", same_core).astype(f32).sum(axis=0)
    new_first = beta_first * first_moment + (1.0 - beta_first) * gradient
    new_second = beta_second * second_moment + (1.0 - beta_second) * gradient * gradient
    corrected_first = new_first / (1.0 - beta_first**STEP)
    corrected_second = new_second / (1.0 - beta_second**STEP)
    update = (corrected_first / (jnp.sqrt(corrected_second) + epsilon)).astype(bf16)
    own_rows = copies_to_all(update, "dp", chips, same_core).reshape(rank // 2, columns)
    other_rows = lax.ppermute(own_rows, "dp", partner)
    place = jnp.arange(rank, dtype=jnp.int32)
    side = place // (rank // 2)
    within = place % (rank // 2)
    source = (
        within // owned * (2 * owned)
        + jnp.where(side == 0, core, 1 - core) * owned
        + within % owned
    )
    pick = (place[:, None] == source[None, :]).astype(bf16)
    ordered = jnp.dot(local_basis, pick, preferred_element_type=f32).astype(bf16)
    expanded = jnp.dot(ordered[:, : rank // 2], own_rows, preferred_element_type=f32)
    expanded = expanded + jnp.dot(ordered[:, rank // 2 :], other_rows, preferred_element_type=f32)
    weight_step = (-expanded).astype(bf16)
    return (new_first, new_second, weight_step)


def solution(mesh):
    in_specs = (
        P("dp", "tensor"),
        P("dp", "tensor"),
        P("tensor", None),
        P("dp", "tensor"),
        P("dp", "tensor"),
        P("dp"),
    )
    out_specs = (P("dp", "tensor"), P("dp", "tensor"), P("dp", "tensor"))
    return jax.shard_map(body, mesh=mesh, in_specs=in_specs, out_specs=out_specs, check_vma=False)
```

profile of v0, /device:TPU:62, one launch (start us, length us, event | category | flops | bytes accessed | tf_op | source)
XLA Modules:
  0.0 160.9 jit_solution(582919417251868514)
XLA Ops:
  0.6 0.0 copy-start
  0.6 0.0 copy-start.4
  0.7 2.6 %convolution_convert_fusion.1 = bf16[512,512]{1,0:T(8,128)(2,1)} fusion(bf16[512,512]{1,0:T(8,128)(2,1)} %param.8, bf16[512,512]{1,0:T(8,128)(2,1)} %param.6), kind=kOutput, calls=%fused_computation.6 | convolution fusion | flops 268697600 | bytes 1572864 | tf_op jit(solution)/shard_map/dot_general | solution.py:58
  3.3 15.2 %all-to-all-start = ((bf16[16,32,512]{2,1,0:T(8,128)(2,1)}), bf16[16,32,512]{2,1,0:T(8,128)(2,1)S(1)}, u32[]{:S(2)}, u32[]{:S(2)}) async-start(bf16[16,32,512]{2,1,0:T(8,128)(2,1)} %bitcast), calls=%async_computation | async-start | bytes 1048576 | tf_op jit(solution)/shard_map/all_to_all | solution.py:16
  18.5 0.0 copy-done.4
  18.5 0.1 select_bitcast_fusion
  18.6 28.4 %all-to-all-done = bf16[16,32,512]{2,1,0:T(8,128)(2,1)S(1)} async-done(((bf16[16,32,512]{2,1,0:T(8,128)(2,1)}), bf16[16,32,512]{2,1,0:T(8,128)(2,1)S(1)}, u32[]{:S(2)}, u32[]{:S(2)}) %all-to-all-start) | async-done | bytes 524320 | tf_op jit(solution)/shard_map/all_to_all | solution.py:16
  47.0 0.1 convert_reduce_fusion.1
  47.1 30.8 %all_gather.3 = bf16[512,512]{1,0:T(8,128)(2,1)S(1)} all-gather(bf16[32,512]{1,0:T(8,128)(2,1)S(1)} %multiply_convert_fusion), channel_id=1, replica_groups=mesh['dp'=32,'tensor'=16] {'tensor'}, dimensions={0}, use_global_device_ids=true | all-gather | bytes 557056 | tf_op jit(solution)/shard_map/all_gather | solution.py:64
  77.9 0.0 copy-done
  77.9 0.6 convolution_convert_fusion
  78.5 1.9 %collective-permute-start = (bf16[256,1792]{1,0:T(8,128)(2,1)S(1)}, bf16[256,1792]{1,0:T(8,128)(2,1)S(1)}, u32[]{:S(2)}, u32[]{:S(2)}) collective-permute-start(bf16[256,1792]{1,0:T(8,128)(2,1)S(1)} %convolution_convert_fusion), channel_id=1, source_target_pairs={{0,16},{16,0},{32,48},{48,32},{64,80},{80,64},{96,112},{112,96},{1... | collective-permute-start | bytes 2752520 | tf_op jit(solution)/shard_map/ppermute | solution.py:71
  80.5 2.4 %collective-permute-done = bf16[256,1792]{1,0:T(8,128)(2,1)S(1)} collective-permute-done((bf16[256,1792]{1,0:T(8,128)(2,1)S(1)}, bf16[256,1792]{1,0:T(8,128)(2,1)S(1)}, u32[]{:S(2)}, u32[]{:S(2)}) %collective-permute-start) | collective-permute-done | bytes 917536 | tf_op jit(solution)/shard_map/ppermute | solution.py:71
  82.9 0.6 add_convert_fusion
  83.5 0.0 copy-start.2
  83.6 0.0 copy-start.3
  83.6 19.0 %all_to_all.15 = bf16[16,16,1792]{2,1,0:T(8,128)(2,1)S(1)} all-to-all(bf16[16,16,1792]{2,1,0:T(8,128)(2,1)S(1)} %bitcast.19), channel_id=1, replica_groups={{0,32,64,96,128,160,192,224,256,288,320,352,384,416,448,480},{16,48,80,..., dimensions={0} | all-to-all | bytes 1835008 | tf_op jit(solution)/shard_map/all_to_all | solution.py:16
  102.6 0.1 convert_reduce_fusion
  102.7 0.0 copy-done.2
  102.7 0.0 copy-done.3
  102.7 0.0 copy-start.1
  102.7 0.7 divide_convert_fusion
  103.5 0.1 broadcast_in_dim.32
  103.5 18.3 %all_to_all.16 = bf16[16,16,1792]{2,1,0:T(8,128)(2,1)S(1)} all-to-all(bf16[16,16,1792]{2,1,0:T(8,128)(2,1)S(1)} %broadcast_in_dim.32), channel_id=1, replica_groups={{0,32,64,96,128,160,192,224,256,288,320,352,384,416,448,480},{16,48,80,..., dimensions={0} | all-to-all | bytes 1835008 | tf_op jit(solution)/shard_map/all_to_all | solution.py:16
  121.8 1.9 %collective-permute-start.2 = (bf16[256,1792]{1,0:T(8,128)(2,1)S(1)}, bf16[256,1792]{1,0:T(8,128)(2,1)}, u32[]{:S(2)}, u32[]{:S(2)}) collective-permute-start(bf16[256,1792]{1,0:T(8,128)(2,1)S(1)} %bitcast.17), channel_id=1, source_target_pairs={{0,16},{16,0},{32,48},{48,32},{64,80},{80,64},{96,112},{112,96},{1... | collective-permute-start | bytes 2752520 | tf_op jit(solution)/shard_map/ppermute | solution.py:81
  123.7 0.0 copy-done.1
  123.8 8.3 %collective-permute-start.1 = (bf16[256,512]{1,0:T(8,128)(2,1)S(1)}, bf16[256,512]{1,0:T(8,128)(2,1)S(1)}, u32[]{:S(2)}, u32[]{:S(2)}) collective-permute-start(bf16[256,512]{1,0:T(8,128)(2,1)S(1)} %constant_dynamic-slice_fusion), channel_id=1, source_target_pairs={{0,0},{1,47},{2,78},{3,109},{4,140},{5,171},{6,202},{7,233},{8,264... | collective-permute-start | bytes 786440 | tf_op jit(solution)/shard_map/ppermute | solution.py:57
  132.1 25.5 %collective-permute-done.1 = bf16[256,512]{1,0:T(8,128)(2,1)S(1)} collective-permute-done((bf16[256,512]{1,0:T(8,128)(2,1)S(1)}, bf16[256,512]{1,0:T(8,128)(2,1)S(1)}, u32[]{:S(2)}, u32[]{:S(2)}) %collective-permute-start.1) | collective-permute-done | bytes 262176 | tf_op jit(solution)/shard_map/ppermute | solution.py:57
  157.6 0.4 convolution_convert_fusion.2
  157.9 0.4 fusion.4
  158.4 0.0 collective-permute-done.2
  158.4 2.5 %fusion.1 = bf16[256,1792]{1,0:T(8,128)(2,1)} fusion(f32[256,1792]{1,0:T(8,128)S(1)} %fusion.4, bf16[256,1792]{1,0:T(8,128)(2,1)} %collective-permute-done.2, bf16[256,512]{1,0:T(8,128)(2,1)S(1)} %convolution_convert_fusion.2), kind=kOutput, calls=%fused_computation.3 | convolution fusion | flops 236257280 | bytes 3801088 | tf_op jit(solution)/shard_map/dot_general | solution.py:93
  (5 shorter events, 0.1 us)
Async XLA Ops:
  0.6 77.2 %copy-start = (bf16[512,1792]{1,0:T(8,128)(2,1)S(1)}, bf16[512,1792]{1,0:T(8,128)(2,1)}, u32[]{:S(2)}) copy-start(bf16[512,1792]{1,0:T(8,128)(2,1)} %param.7) | copy-start | bytes 5505028
  0.6 17.8 %copy-start.4 = (s32[4]{0:T(128)S(1)}, s32[4]{0:T(128)}, u32[]{:S(2)}) copy-start(s32[4]{0:T(128)} %param.11) | copy-start | bytes 52
  3.3 43.7 %all-to-all-start = ((bf16[16,32,512]{2,1,0:T(8,128)(2,1)}), bf16[16,32,512]{2,1,0:T(8,128)(2,1)S(1)}, u32[]{:S(2)}, u32[]{:S(2)}) async-start(bf16[16,32,512]{2,1,0:T(8,128)(2,1)} %bitcast), calls=%async_computation | async-start | bytes 1048576 | tf_op jit(solution)/shard_map/all_to_all | solution.py:16
  78.5 4.4 %collective-permute-start = (bf16[256,1792]{1,0:T(8,128)(2,1)S(1)}, bf16[256,1792]{1,0:T(8,128)(2,1)S(1)}, u32[]{:S(2)}, u32[]{:S(2)}) collective-permute-start(bf16[256,1792]{1,0:T(8,128)(2,1)S(1)} %convolution_convert_fusion), channel_id=1, source_target_pairs={{0,16},{16,0},{32,48},{48,32},{64,80},{80,64},{96,112},{112,96},{1... | collective-permute-start | bytes 2752520 | tf_op jit(solution)/shard_map/ppermute | solution.py:71
  83.5 19.2 %copy-start.2 = (f32[16,1792]{1,0:T(8,128)S(1)}, f32[16,1792]{1,0:T(8,128)}, u32[]{:S(2)}) copy-start(f32[16,1792]{1,0:T(8,128)} %param.10) | copy-start | bytes 344068
  83.6 19.1 %copy-start.3 = (f32[16,1792]{1,0:T(8,128)S(1)}, f32[16,1792]{1,0:T(8,128)}, u32[]{:S(2)}) copy-start(f32[16,1792]{1,0:T(8,128)} %param.9) | copy-start | bytes 344068
  102.7 21.0 %copy-start.1 = (bf16[512,512]{1,0:T(8,128)(2,1)S(1)}, bf16[512,512]{1,0:T(8,128)(2,1)}, u32[]{:S(2)}) copy-start(bf16[512,512]{1,0:T(8,128)(2,1)} %param.8) | copy-start | bytes 1572868
  121.8 36.6 %collective-permute-start.2 = (bf16[256,1792]{1,0:T(8,128)(2,1)S(1)}, bf16[256,1792]{1,0:T(8,128)(2,1)}, u32[]{:S(2)}, u32[]{:S(2)}) collective-permute-start(bf16[256,1792]{1,0:T(8,128)(2,1)S(1)} %bitcast.17), channel_id=1, source_target_pairs={{0,16},{16,0},{32,48},{48,32},{64,80},{80,64},{96,112},{112,96},{1... | collective-permute-start | bytes 2752520 | tf_op jit(solution)/shard_map/ppermute | solution.py:81
  123.8 33.8 %collective-permute-start.1 = (bf16[256,512]{1,0:T(8,128)(2,1)S(1)}, bf16[256,512]{1,0:T(8,128)(2,1)S(1)}, u32[]{:S(2)}, u32[]{:S(2)}) collective-permute-start(bf16[256,512]{1,0:T(8,128)(2,1)S(1)} %constant_dynamic-slice_fusion), channel_id=1, source_target_pairs={{0,0},{1,47},{2,78},{3,109},{4,140},{5,171},{6,202},{7,233},{8,264... | collective-permute-start | bytes 786440 | tf_op jit(solution)/shard_map/ppermute | solution.py:57
where the time goes:
time: 161 us
  blocking collectives  68 us (42%)
  waiting for transfers between devices  56.3 us (35%)
  starting transfers between devices  27.3 us (17%)
  matrix products  7.21 us (4%)
    all_to_all x2, blocking collectives, exchange(): lax.all_to_all(tiles, axis, split_axis=0, concat_axis=0, tiled=True, axis...  37.3 us
    all_gather x1, blocking collectives, body(): weighted = lax.all_gather(weighted, 'tensor', axis=0, tiled=True)  30.8 us
    all_to_all x1, waiting for transfers between devices, exchange(): lax.all_to_all(tiles, axis, split_axis=0, concat_axis=0, tiled=True, axis...  28.4 us
    ppermute x1, waiting for transfers between devices, body(): lax.ppermute(half_block, ('dp', 'tensor'), basis_routes(chips, splits))  25.5 us
    all_to_all x1, starting transfers between devices, exchange(): lax.all_to_all(tiles, axis, split_axis=0, concat_axis=0, tiled=True, axis...  15.2 us
    ppermute x1, starting transfers between devices, body(): lax.ppermute(half_block, ('dp', 'tensor'), basis_routes(chips, splits))  8.29 us
  transfers between devices with their start and end apart: 4, of which 3 were waited for; matrix products, arithmetic and copies ran while one was open for 1% of the time, Pallas kernels for 0%

commit v1 on v0

--- a/solution.py
+++ b/solution.py
@@ -10,6 +10,28 @@
 epsilon = 1e-08
 bf16 = jnp.bfloat16
 f32 = jnp.float32
+
+
+def laid_out(pieces, dim):
+    pieces = jnp.moveaxis(pieces, 0, dim)
+    lengths = pieces.shape
+    return pieces.reshape(*lengths[:dim], lengths[dim] * lengths[dim + 1], *lengths[dim + 2 :])
+
+
+def collect(value, axis, dim):
+    peers = lax.axis_size(axis)
+    pairs = [(i, (i + 1) % peers) for i in range(peers)]
+    back = [(b, a) for a, b in pairs]
+    lower, upper = ([], [])
+    for turn in range(peers - 1):
+        if turn % 2 == 0:
+            lower.append(lax.ppermute(lower[-1] if lower else value, axis, pairs))
+        else:
+            upper.append(lax.ppermute(upper[-1] if upper else value, axis, back))
+    blocks = jnp.stack([*lower[::-1], value, *upper])
+    shift = lax.axis_index(axis) - len(lower)
+    blocks = blocks[(jnp.arange(peers) - shift) % peers]
+    return laid_out(blocks, dim)
 
 
 def exchange(tiles, axis, groups=None):
@@ -61,7 +83,7 @@
     arrived = exchange(partial.reshape(splits, rank // splits, slots), "tensor")
     coordinates = arrived.astype(f32).sum(axis=0)
     weighted = (coordinates * token_weights(list_lengths)[None, :]).astype(bf16)
-    weighted = lax.all_gather(weighted, "tensor", axis=0, tiled=True)
+    weighted = collect(weighted, "tensor", 0)
     by_owner = weighted.reshape(chips, 2, owned, slots)
     other = lax.dynamic_index_in_dim(by_owner, 1 - core, 1, keepdims=False).reshape(
         rank // 2, slots

time: 161 us -> 191 us (1.19)
  starting transfers between devices: 27.3 us -> 80.6 us
  blocking collectives: 68 us -> 37.2 us
  waiting for transfers between devices: 56.3 us -> 61.6 us
    ppermute x0 -> x15, starting transfers between devices: none -> 51.6 us  [the longest x7 35.5 us: collect(): upper.append(lax.ppermute(upper[-1] if upper else value, axis, back))]
    all_gather x1 -> x0, blocking collectives: 30.8 us -> none  [body(): weighted = lax.all_gather(weighted, 'tensor', axis=0, tiled=True)]
    ppermute x0 -> x15, waiting for transfers between devices: none -> 5.16 us  [the longest x8 3.77 us: collect(): lower.append(lax.ppermute(lower[-1] if lower else value, axis, pairs))]
  transfers between devices with their start and end apart: 4 -> 19, of which waited for: 3 -> 5; matrix products, arithmetic and copies ran while one was open for 1% -> 1% of each run, Pallas kernels for 0% -> 0%
where the time goes in v1:
time: 191 us; the launch traced here: 190 us
  starting transfers between devices  80.6 us (42%)
  waiting for transfers between devices  61.6 us (32%)
  blocking collectives  37.2 us (19%)
  matrix products  7.21 us (4%)
    all_to_all x2, blocking collectives, exchange(): lax.all_to_all(tiles, axis, split_axis=0, concat_axis=0, tiled=True, axis...  37.2 us
    ppermute x7, starting transfers between devices, collect(): upper.append(lax.ppermute(upper[-1] if upper else value, axis, back))  35.5 us
    all_to_all x1, waiting for transfers between devices, exchange(): lax.all_to_all(tiles, axis, split_axis=0, concat_axis=0, tiled=True, axis...  28.4 us
    ppermute x1, waiting for transfers between devices, body(): lax.ppermute(half_block, ('dp', 'tensor'), basis_routes(chips, splits))  25.5 us
    ppermute x8, starting transfers between devices, collect(): lower.append(lax.ppermute(lower[-1] if lower else value, axis, pairs))  16 us
    all_to_all x1, starting transfers between devices, exchange(): lax.all_to_all(tiles, axis, split_axis=0, concat_axis=0, tiled=True, axis...  15.2 us
    ppermute x1, starting transfers between devices, body(): lax.ppermute(half_block, ('dp', 'tensor'), basis_routes(chips, splits))  9.95 us
  transfers between devices with their start and end apart: 19, of which 5 were waited for; matrix products, arithmetic and copies ran while one was open for 1% of the time, Pallas kernels for 0%

profile of v1, /device:TPU:62, one launch (start us, length us, event | category | flops | bytes accessed | tf_op | source)
XLA Modules:
  0.0 189.6 jit_solution(13228799988692870)
XLA Ops:
  0.7 2.6 %convolution_convert_fusion.1 = bf16[512,512]{1,0:T(8,128)(2,1)} fusion(bf16[512,512]{1,0:T(8,128)(2,1)} %param.8, bf16[512,512]{1,0:T(8,128)(2,1)} %param.6), kind=kOutput, calls=%fused_computation.7 | convolution fusion | flops 268697600 | bytes 1572864 | tf_op jit(solution)/shard_map/dot_general | solution.py:80
  3.3 15.2 %all-to-all-start = ((bf16[16,32,512]{2,1,0:T(8,128)(2,1)}), bf16[16,32,512]{2,1,0:T(8,128)(2,1)S(1)}, u32[]{:S(2)}, u32[]{:S(2)}) async-start(bf16[16,32,512]{2,1,0:T(8,128)(2,1)} %bitcast), calls=%async_computation | async-start | bytes 1048576 | tf_op jit(solution)/shard_map/all_to_all | solution.py:38
  18.6 28.4 %all-to-all-done = bf16[16,32,512]{2,1,0:T(8,128)(2,1)S(1)} async-done(((bf16[16,32,512]{2,1,0:T(8,128)(2,1)}), bf16[16,32,512]{2,1,0:T(8,128)(2,1)S(1)}, u32[]{:S(2)}, u32[]{:S(2)}) %all-to-all-start) | async-done | bytes 524320 | tf_op jit(solution)/shard_map/all_to_all | solution.py:38
  47.1 2.1 %collective-permute-start = (bf16[32,512]{1,0:T(8,128)(2,1)S(1)}, bf16[32,512]{1,0:T(8,128)(2,1)S(1)}, u32[]{:S(2)}, u32[]{:S(2)}) collective-permute-start(bf16[32,512]{1,0:T(8,128)(2,1)S(1)} %multiply_convert_fusion), channel_id=1, source_target_pairs={{0,1},{1,2},{2,3},{3,4},{4,5},{5,6},{6,7},{7,8},{8,9},{9,10},{10,1... | collective-permute-start | bytes 98312 | tf_op jit(solution)/shard_map/ppermute | solution.py:28
  49.2 3.8 %collective-permute-done = bf16[32,512]{1,0:T(8,128)(2,1)S(1)} collective-permute-done((bf16[32,512]{1,0:T(8,128)(2,1)S(1)}, bf16[32,512]{1,0:T(8,128)(2,1)S(1)}, u32[]{:S(2)}, u32[]{:S(2)}) %collective-permute-start) | collective-permute-done | bytes 32800 | tf_op jit(solution)/shard_map/ppermute | solution.py:28
  52.9 2.4 %collective-permute-start.1 = (bf16[32,512]{1,0:T(8,128)(2,1)S(1)}, bf16[32,512]{1,0:T(8,128)(2,1)S(1)}, u32[]{:S(2)}, u32[]{:S(2)}) collective-permute-start(bf16[32,512]{1,0:T(8,128)(2,1)S(1)} %collective-permute-done), channel_id=1, source_target_pairs={{0,1},{1,2},{2,3},{3,4},{4,5},{5,6},{6,7},{7,8},{8,9},{9,10},{10,1... | collective-permute-start | bytes 98312 | tf_op jit(solution)/shard_map/ppermute | solution.py:28
  55.3 4.7 %collective-permute-start.8 = (bf16[32,512]{1,0:T(8,128)(2,1)S(1)}, bf16[32,512]{1,0:T(8,128)(2,1)S(1)}, u32[]{:S(2)}, u32[]{:S(2)}) collective-permute-start(bf16[32,512]{1,0:T(8,128)(2,1)S(1)} %multiply_convert_fusion), channel_id=1, source_target_pairs={{1,0},{2,1},{3,2},{4,3},{5,4},{6,5},{7,6},{8,7},{9,8},{10,9},{11,1... | collective-permute-start | bytes 98312 | tf_op jit(solution)/shard_map/ppermute | solution.py:30
  60.1 1.9 %collective-permute-start.2 = (bf16[32,512]{1,0:T(8,128)(2,1)S(1)}, bf16[32,512]{1,0:T(8,128)(2,1)S(1)}, u32[]{:S(2)}, u32[]{:S(2)}) collective-permute-start(bf16[32,512]{1,0:T(8,128)(2,1)S(1)} %collective-permute-done.1), channel_id=1, source_target_pairs={{0,1},{1,2},{2,3},{3,4},{4,5},{5,6},{6,7},{7,8},{8,9},{9,10},{10,1... | collective-permute-start | bytes 98312 | tf_op jit(solution)/shard_map/ppermute | solution.py:28
  62.0 5.1 %collective-permute-start.9 = (bf16[32,512]{1,0:T(8,128)(2,1)S(1)}, bf16[32,512]{1,0:T(8,128)(2,1)S(1)}, u32[]{:S(2)}, u32[]{:S(2)}) collective-permute-start(bf16[32,512]{1,0:T(8,128)(2,1)S(1)} %collective-permute-done.8), channel_id=1, source_target_pairs={{1,0},{2,1},{3,2},{4,3},{5,4},{6,5},{7,6},{8,7},{9,8},{10,9},{11,1... | collective-permute-start | bytes 98312 | tf_op jit(solution)/shard_map/ppermute | solution.py:30
  67.2 1.9 %collective-permute-start.3 = (bf16[32,512]{1,0:T(8,128)(2,1)S(1)}, bf16[32,512]{1,0:T(8,128)(2,1)S(1)}, u32[]{:S(2)}, u32[]{:S(2)}) collective-permute-start(bf16[32,512]{1,0:T(8,128)(2,1)S(1)} %collective-permute-done.2), channel_id=1, source_target_pairs={{0,1},{1,2},{2,3},{3,4},{4,5},{5,6},{6,7},{7,8},{8,9},{9,10},{10,1... | collective-permute-start | bytes 98312 | tf_op jit(solution)/shard_map/ppermute | solution.py:28
  69.1 5.1 %collective-permute-start.10 = (bf16[32,512]{1,0:T(8,128)(2,1)S(1)}, bf16[32,512]{1,0:T(8,128)(2,1)S(1)}, u32[]{:S(2)}, u32[]{:S(2)}) collective-permute-start(bf16[32,512]{1,0:T(8,128)(2,1)S(1)} %collective-permute-done.9), channel_id=1, source_target_pairs={{1,0},{2,1},{3,2},{4,3},{5,4},{6,5},{7,6},{8,7},{9,8},{10,9},{11,1... | collective-permute-start | bytes 98312 | tf_op jit(solution)/shard_map/ppermute | solution.py:30
  74.3 1.9 %collective-permute-start.4 = (bf16[32,512]{1,0:T(8,128)(2,1)S(1)}, bf16[32,512]{1,0:T(8,128)(2,1)S(1)}, u32[]{:S(2)}, u32[]{:S(2)}) collective-permute-start(bf16[32,512]{1,0:T(8,128)(2,1)S(1)} %collective-permute-done.3), channel_id=1, source_target_pairs={{0,1},{1,2},{2,3},{3,4},{4,5},{5,6},{6,7},{7,8},{8,9},{9,10},{10,1... | collective-permute-start | bytes 98312 | tf_op jit(solution)/shard_map/ppermute | solution.py:28
  76.2 5.1 %collective-permute-start.11 = (bf16[32,512]{1,0:T(8,128)(2,1)S(1)}, bf16[32,512]{1,0:T(8,128)(2,1)S(1)}, u32[]{:S(2)}, u32[]{:S(2)}) collective-permute-start(bf16[32,512]{1,0:T(8,128)(2,1)S(1)} %collective-permute-done.10), channel_id=1, source_target_pairs={{1,0},{2,1},{3,2},{4,3},{5,4},{6,5},{7,6},{8,7},{9,8},{10,9},{11,1... | collective-permute-start | bytes 98312 | tf_op jit(solution)/shard_map/ppermute | solution.py:30
  81.4 1.9 %collective-permute-start.5 = (bf16[32,512]{1,0:T(8,128)(2,1)S(1)}, bf16[32,512]{1,0:T(8,128)(2,1)S(1)}, u32[]{:S(2)}, u32[]{:S(2)}) collective-permute-start(bf16[32,512]{1,0:T(8,128)(2,1)S(1)} %collective-permute-done.4), channel_id=1, source_target_pairs={{0,1},{1,2},{2,3},{3,4},{4,5},{5,6},{6,7},{7,8},{8,9},{9,10},{10,1... | collective-permute-start | bytes 98312 | tf_op jit(solution)/shard_map/ppermute | solution.py:28
  83.3 5.1 %collective-permute-start.12 = (bf16[32,512]{1,0:T(8,128)(2,1)S(1)}, bf16[32,512]{1,0:T(8,128)(2,1)S(1)}, u32[]{:S(2)}, u32[]{:S(2)}) collective-permute-start(bf16[32,512]{1,0:T(8,128)(2,1)S(1)} %collective-permute-done.11), channel_id=1, source_target_pairs={{1,0},{2,1},{3,2},{4,3},{5,4},{6,5},{7,6},{8,7},{9,8},{10,9},{11,1... | collective-permute-start | bytes 98312 | tf_op jit(solution)/shard_map/ppermute | solution.py:30
  88.5 1.9 %collective-permute-start.6 = (bf16[32,512]{1,0:T(8,128)(2,1)S(1)}, bf16[32,512]{1,0:T(8,128)(2,1)S(1)}, u32[]{:S(2)}, u32[]{:S(2)}) collective-permute-start(bf16[32,512]{1,0:T(8,128)(2,1)S(1)} %collective-permute-done.5), channel_id=1, source_target_pairs={{0,1},{1,2},{2,3},{3,4},{4,5},{5,6},{6,7},{7,8},{8,9},{9,10},{10,1... | collective-permute-start | bytes 98312 | tf_op jit(solution)/shard_map/ppermute | solution.py:28
  90.4 5.1 %collective-permute-start.13 = (bf16[32,512]{1,0:T(8,128)(2,1)S(1)}, bf16[32,512]{1,0:T(8,128)(2,1)S(1)}, u32[]{:S(2)}, u32[]{:S(2)}) collective-permute-start(bf16[32,512]{1,0:T(8,128)(2,1)S(1)} %collective-permute-done.12), channel_id=1, source_target_pairs={{1,0},{2,1},{3,2},{4,3},{5,4},{6,5},{7,6},{8,7},{9,8},{10,9},{11,1... | collective-permute-start | bytes 98312 | tf_op jit(solution)/shard_map/ppermute | solution.py:30
  95.6 1.9 %collective-permute-start.7 = (bf16[32,512]{1,0:T(8,128)(2,1)S(1)}, bf16[32,512]{1,0:T(8,128)(2,1)S(1)}, u32[]{:S(2)}, u32[]{:S(2)}) collective-permute-start(bf16[32,512]{1,0:T(8,128)(2,1)S(1)} %collective-permute-done.6), channel_id=1, source_target_pairs={{0,1},{1,2},{2,3},{3,4},{4,5},{5,6},{6,7},{7,8},{8,9},{9,10},{10,1... | collective-permute-start | bytes 98312 | tf_op jit(solution)/shard_map/ppermute | solution.py:28
  97.6 5.1 %collective-permute-start.14 = (bf16[32,512]{1,0:T(8,128)(2,1)S(1)}, bf16[32,512]{1,0:T(8,128)(2,1)S(1)}, u32[]{:S(2)}, u32[]{:S(2)}) collective-permute-start(bf16[32,512]{1,0:T(8,128)(2,1)S(1)} %collective-permute-done.13), channel_id=1, source_target_pairs={{1,0},{2,1},{3,2},{4,3},{5,4},{6,5},{7,6},{8,7},{9,8},{10,9},{11,1... | collective-permute-start | bytes 98312 | tf_op jit(solution)/shard_map/ppermute | solution.py:30
  102.9 1.4 collective-permute-done.14
  104.3 0.6 gather_fusion
  104.9 0.6 convolution_convert_fusion
  105.6 1.9 %collective-permute-start.15 = (bf16[256,1792]{1,0:T(8,128)(2,1)S(1)}, bf16[256,1792]{1,0:T(8,128)(2,1)S(1)}, u32[]{:S(2)}, u32[]{:S(2)}) collective-permute-start(bf16[256,1792]{1,0:T(8,128)(2,1)S(1)} %convolution_convert_fusion), channel_id=1, source_target_pairs={{0,16},{16,0},{32,48},{48,32},{64,80},{80,64},{96,112},{112,96},{1... | collective-permute-start | bytes 2752520 | tf_op jit(solution)/shard_map/ppermute | solution.py:93
  107.5 2.4 %collective-permute-done.15 = bf16[256,1792]{1,0:T(8,128)(2,1)S(1)} collective-permute-done((bf16[256,1792]{1,0:T(8,128)(2,1)S(1)}, bf16[256,1792]{1,0:T(8,128)(2,1)S(1)}, u32[]{:S(2)}, u32[]{:S(2)}) %collective-permute-start.15) | collective-permute-done | bytes 917536 | tf_op jit(solution)/shard_map/ppermute | solution.py:93
  109.9 0.6 add_convert_fusion
  110.6 19.0 %all_to_all.15 = bf16[16,16,1792]{2,1,0:T(8,128)(2,1)S(1)} all-to-all(bf16[16,16,1792]{2,1,0:T(8,128)(2,1)S(1)} %bitcast.57), channel_id=1, replica_groups={{0,32,64,96,128,160,192,224,256,288,320,352,384,416,448,480},{16,48,80,..., dimensions={0} | all-to-all | bytes 1835008 | tf_op jit(solution)/shard_map/all_to_all | solution.py:38
  129.8 0.7 divide_convert_fusion
  130.6 18.3 %all_to_all.16 = bf16[16,16,1792]{2,1,0:T(8,128)(2,1)S(1)} all-to-all(bf16[16,16,1792]{2,1,0:T(8,128)(2,1)S(1)} %broadcast_in_dim.33), channel_id=1, replica_groups={{0,32,64,96,128,160,192,224,256,288,320,352,384,416,448,480},{16,48,80,..., dimensions={0} | all-to-all | bytes 1835008 | tf_op jit(solution)/shard_map/all_to_all | solution.py:38
  148.8 1.9 %collective-permute-start.17 = (bf16[256,1792]{1,0:T(8,128)(2,1)S(1)}, bf16[256,1792]{1,0:T(8,128)(2,1)}, u32[]{:S(2)}, u32[]{:S(2)}) collective-permute-start(bf16[256,1792]{1,0:T(8,128)(2,1)S(1)} %bitcast.55), channel_id=1, source_target_pairs={{0,16},{16,0},{32,48},{48,32},{64,80},{80,64},{96,112},{112,96},{1... | collective-permute-start | bytes 2752520 | tf_op jit(solution)/shard_map/ppermute | solution.py:103
  150.8 9.9 %collective-permute-start.16 = (bf16[256,512]{1,0:T(8,128)(2,1)S(1)}, bf16[256,512]{1,0:T(8,128)(2,1)S(1)}, u32[]{:S(2)}, u32[]{:S(2)}) collective-permute-start(bf16[256,512]{1,0:T(8,128)(2,1)S(1)} %constant_dynamic-slice_fusion), channel_id=1, source_target_pairs={{0,0},{1,47},{2,78},{3,109},{4,140},{5,171},{6,202},{7,233},{8,264... | collective-permute-start | bytes 786440 | tf_op jit(solution)/shard_map/ppermute | solution.py:79
  160.8 25.5 %collective-permute-done.16 = bf16[256,512]{1,0:T(8,128)(2,1)S(1)} collective-permute-done((bf16[256,512]{1,0:T(8,128)(2,1)S(1)}, bf16[256,512]{1,0:T(8,128)(2,1)S(1)}, u32[]{:S(2)}, u32[]{:S(2)}) %collective-permute-start.16) | collective-permute-done | bytes 262176 | tf_op jit(solution)/shard_map/ppermute | solution.py:79
  187.1 2.5 %fusion.1 = bf16[256,1792]{1,0:T(8,128)(2,1)} fusion(f32[256,1792]{1,0:T(8,128)S(1)} %fusion.4, bf16[256,1792]{1,0:T(8,128)(2,1)} %collective-permute-done.17, bf16[256,512]{1,0:T(8,128)(2,1)S(1)} %convolution_convert_fusion.2), kind=kOutput, calls=%fused_computation.4 | convolution fusion | flops 236257280 | bytes 3801088 | tf_op jit(solution)/shard_map/dot_general | solution.py:115
  (53 shorter events, 1.4 us)
Async XLA Ops:
  0.6 104.3 %copy-start = (bf16[512,1792]{1,0:T(8,128)(2,1)S(1)}, bf16[512,1792]{1,0:T(8,128)(2,1)}, u32[]{:S(2)}) copy-start(bf16[512,1792]{1,0:T(8,128)(2,1)} %param.7) | copy-start | bytes 5505028
  0.6 17.8 %copy-start.4 = (s32[4]{0:T(128)S(1)}, s32[4]{0:T(128)}, u32[]{:S(2)}) copy-start(s32[4]{0:T(128)} %param.11) | copy-start | bytes 52
  3.3 43.7 %all-to-all-start = ((bf16[16,32,512]{2,1,0:T(8,128)(2,1)}), bf16[16,32,512]{2,1,0:T(8,128)(2,1)S(1)}, u32[]{:S(2)}, u32[]{:S(2)}) async-start(bf16[16,32,512]{2,1,0:T(8,128)(2,1)} %bitcast), calls=%async_computation | async-start | bytes 1048576 | tf_op jit(solution)/shard_map/all_to_all | solution.py:38
  47.1 5.8 %collective-permute-start = (bf16[32,512]{1,0:T(8,128)(2,1)S(1)}, bf16[32,512]{1,0:T(8,128)(2,1)S(1)}, u32[]{:S(2)}, u32[]{:S(2)}) collective-permute-start(bf16[32,512]{1,0:T(8,128)(2,1)S(1)} %multiply_convert_fusion), channel_id=1, source_target_pairs={{0,1},{1,2},{2,3},{3,4},{4,5},{5,6},{6,7},{7,8},{8,9},{9,10},{10,1... | collective-permute-start | bytes 98312 | tf_op jit(solution)/shard_map/ppermute | solution.py:28
  52.9 7.2 %collective-permute-start.1 = (bf16[32,512]{1,0:T(8,128)(2,1)S(1)}, bf16[32,512]{1,0:T(8,128)(2,1)S(1)}, u32[]{:S(2)}, u32[]{:S(2)}) collective-permute-start(bf16[32,512]{1,0:T(8,128)(2,1)S(1)} %collective-permute-done), channel_id=1, source_target_pairs={{0,1},{1,2},{2,3},{3,4},{4,5},{5,6},{6,7},{7,8},{8,9},{9,10},{10,1... | collective-permute-start | bytes 98312 | tf_op jit(solution)/shard_map/ppermute | solution.py:28
  55.3 6.7 %collective-permute-start.8 = (bf16[32,512]{1,0:T(8,128)(2,1)S(1)}, bf16[32,512]{1,0:T(8,128)(2,1)S(1)}, u32[]{:S(2)}, u32[]{:S(2)}) collective-permute-start(bf16[32,512]{1,0:T(8,128)(2,1)S(1)} %multiply_convert_fusion), channel_id=1, source_target_pairs={{1,0},{2,1},{3,2},{4,3},{5,4},{6,5},{7,6},{8,7},{9,8},{10,9},{11,1... | collective-permute-start | bytes 98312 | tf_op jit(solution)/shard_map/ppermute | solution.py:30
  60.1 7.1 %collective-permute-start.2 = (bf16[32,512]{1,0:T(8,128)(2,1)S(1)}, bf16[32,512]{1,0:T(8,128)(2,1)S(1)}, u32[]{:S(2)}, u32[]{:S(2)}) collective-permute-start(bf16[32,512]{1,0:T(8,128)(2,1)S(1)} %collective-permute-done.1), channel_id=1, source_target_pairs={{0,1},{1,2},{2,3},{3,4},{4,5},{5,6},{6,7},{7,8},{8,9},{9,10},{10,1... | collective-permute-start | bytes 98312 | tf_op jit(solution)/shard_map/ppermute | solution.py:28
  62.0 7.1 %collective-permute-start.9 = (bf16[32,512]{1,0:T(8,128)(2,1)S(1)}, bf16[32,512]{1,0:T(8,128)(2,1)S(1)}, u32[]{:S(2)}, u32[]{:S(2)}) collective-permute-start(bf16[32,512]{1,0:T(8,128)(2,1)S(1)} %collective-permute-done.8), channel_id=1, source_target_pairs={{1,0},{2,1},{3,2},{4,3},{5,4},{6,5},{7,6},{8,7},{9,8},{10,9},{11,1... | collective-permute-start | bytes 98312 | tf_op jit(solution)/shard_map/ppermute | solution.py:30
  67.2 7.1 %collective-permute-start.3 = (bf16[32,512]{1,0:T(8,128)(2,1)S(1)}, bf16[32,512]{1,0:T(8,128)(2,1)S(1)}, u32[]{:S(2)}, u32[]{:S(2)}) collective-permute-start(bf16[32,512]{1,0:T(8,128)(2,1)S(1)} %collective-permute-done.2), channel_id=1, source_target_pairs={{0,1},{1,2},{2,3},{3,4},{4,5},{5,6},{6,7},{7,8},{8,9},{9,10},{10,1... | collective-permute-start | bytes 98312 | tf_op jit(solution)/shard_map/ppermute | solution.py:28
  69.1 7.1 %collective-permute-start.10 = (bf16[32,512]{1,0:T(8,128)(2,1)S(1)}, bf16[32,512]{1,0:T(8,128)(2,1)S(1)}, u32[]{:S(2)}, u32[]{:S(2)}) collective-permute-start(bf16[32,512]{1,0:T(8,128)(2,1)S(1)} %collective-permute-done.9), channel_id=1, source_target_pairs={{1,0},{2,1},{3,2},{4,3},{5,4},{6,5},{7,6},{8,7},{9,8},{10,9},{11,1... | collective-permute-start | bytes 98312 | tf_op jit(solution)/shard_map/ppermute | solution.py:30
  74.3 7.1 %collective-permute-start.4 = (bf16[32,512]{1,0:T(8,128)(2,1)S(1)}, bf16[32,512]{1,0:T(8,128)(2,1)S(1)}, u32[]{:S(2)}, u32[]{:S(2)}) collective-permute-start(bf16[32,512]{1,0:T(8,128)(2,1)S(1)} %collective-permute-done.3), channel_id=1, source_target_pairs={{0,1},{1,2},{2,3},{3,4},{4,5},{5,6},{6,7},{7,8},{8,9},{9,10},{10,1... | collective-permute-start | bytes 98312 | tf_op jit(solution)/shard_map/ppermute | solution.py:28
  76.2 7.1 %collective-permute-start.11 = (bf16[32,512]{1,0:T(8,128)(2,1)S(1)}, bf16[32,512]{1,0:T(8,128)(2,1)S(1)}, u32[]{:S(2)}, u32[]{:S(2)}) collective-permute-start(bf16[32,512]{1,0:T(8,128)(2,1)S(1)} %collective-permute-done.10), channel_id=1, source_target_pairs={{1,0},{2,1},{3,2},{4,3},{5,4},{6,5},{7,6},{8,7},{9,8},{10,9},{11,1... | collective-permute-start | bytes 98312 | tf_op jit(solution)/shard_map/ppermute | solution.py:30
  81.4 7.1 %collective-permute-start.5 = (bf16[32,512]{1,0:T(8,128)(2,1)S(1)}, bf16[32,512]{1,0:T(8,128)(2,1)S(1)}, u32[]{:S(2)}, u32[]{:S(2)}) collective-permute-start(bf16[32,512]{1,0:T(8,128)(2,1)S(1)} %collective-permute-done.4), channel_id=1, source_target_pairs={{0,1},{1,2},{2,3},{3,4},{4,5},{5,6},{6,7},{7,8},{8,9},{9,10},{10,1... | collective-permute-start | bytes 98312 | tf_op jit(solution)/shard_map/ppermute | solution.py:28
  83.3 7.1 %collective-permute-start.12 = (bf16[32,512]{1,0:T(8,128)(2,1)S(1)}, bf16[32,512]{1,0:T(8,128)(2,1)S(1)}, u32[]{:S(2)}, u32[]{:S(2)}) collective-permute-start(bf16[32,512]{1,0:T(8,128)(2,1)S(1)} %collective-permute-done.11), channel_id=1, source_target_pairs={{1,0},{2,1},{3,2},{4,3},{5,4},{6,5},{7,6},{8,7},{9,8},{10,9},{11,1... | collective-permute-start | bytes 98312 | tf_op jit(solution)/shard_map/ppermute | solution.py:30
  88.5 7.1 %collective-permute-start.6 = (bf16[32,512]{1,0:T(8,128)(2,1)S(1)}, bf16[32,512]{1,0:T(8,128)(2,1)S(1)}, u32[]{:S(2)}, u32[]{:S(2)}) collective-permute-start(bf16[32,512]{1,0:T(8,128)(2,1)S(1)} %collective-permute-done.5), channel_id=1, source_target_pairs={{0,1},{1,2},{2,3},{3,4},{4,5},{5,6},{6,7},{7,8},{8,9},{9,10},{10,1... | collective-permute-start | bytes 98312 | tf_op jit(solution)/shard_map/ppermute | solution.py:28
  90.4 7.1 %collective-permute-start.13 = (bf16[32,512]{1,0:T(8,128)(2,1)S(1)}, bf16[32,512]{1,0:T(8,128)(2,1)S(1)}, u32[]{:S(2)}, u32[]{:S(2)}) collective-permute-start(bf16[32,512]{1,0:T(8,128)(2,1)S(1)} %collective-permute-done.12), channel_id=1, source_target_pairs={{1,0},{2,1},{3,2},{4,3},{5,4},{6,5},{7,6},{8,7},{9,8},{10,9},{11,1... | collective-permute-start | bytes 98312 | tf_op jit(solution)/shard_map/ppermute | solution.py:30
  95.6 7.1 %collective-permute-start.7 = (bf16[32,512]{1,0:T(8,128)(2,1)S(1)}, bf16[32,512]{1,0:T(8,128)(2,1)S(1)}, u32[]{:S(2)}, u32[]{:S(2)}) collective-permute-start(bf16[32,512]{1,0:T(8,128)(2,1)S(1)} %collective-permute-done.6), channel_id=1, source_target_pairs={{0,1},{1,2},{2,3},{3,4},{4,5},{5,6},{6,7},{7,8},{8,9},{9,10},{10,1... | collective-permute-start | bytes 98312 | tf_op jit(solution)/shard_map/ppermute | solution.py:28
  97.6 6.7 %collective-permute-start.14 = (bf16[32,512]{1,0:T(8,128)(2,1)S(1)}, bf16[32,512]{1,0:T(8,128)(2,1)S(1)}, u32[]{:S(2)}, u32[]{:S(2)}) collective-permute-start(bf16[32,512]{1,0:T(8,128)(2,1)S(1)} %collective-permute-done.13), channel_id=1, source_target_pairs={{1,0},{2,1},{3,2},{4,3},{5,4},{6,5},{7,6},{8,7},{9,8},{10,9},{11,1... | collective-permute-start | bytes 98312 | tf_op jit(solution)/shard_map/ppermute | solution.py:30
  105.6 4.4 %collective-permute-start.15 = (bf16[256,1792]{1,0:T(8,128)(2,1)S(1)}, bf16[256,1792]{1,0:T(8,128)(2,1)S(1)}, u32[]{:S(2)}, u32[]{:S(2)}) collective-permute-start(bf16[256,1792]{1,0:T(8,128)(2,1)S(1)} %convolution_convert_fusion), channel_id=1, source_target_pairs={{0,16},{16,0},{32,48},{48,32},{64,80},{80,64},{96,112},{112,96},{1... | collective-permute-start | bytes 2752520 | tf_op jit(solution)/shard_map/ppermute | solution.py:93
  110.6 19.1 %copy-start.2 = (f32[16,1792]{1,0:T(8,128)S(1)}, f32[16,1792]{1,0:T(8,128)}, u32[]{:S(2)}) copy-start(f32[16,1792]{1,0:T(8,128)} %param.10) | copy-start | bytes 344068
  110.6 19.1 %copy-start.3 = (f32[16,1792]{1,0:T(8,128)S(1)}, f32[16,1792]{1,0:T(8,128)}, u32[]{:S(2)}) copy-start(f32[16,1792]{1,0:T(8,128)} %param.9) | copy-start | bytes 344068
  129.7 21.0 %copy-start.1 = (bf16[512,512]{1,0:T(8,128)(2,1)S(1)}, bf16[512,512]{1,0:T(8,128)(2,1)}, u32[]{:S(2)}) copy-start(bf16[512,512]{1,0:T(8,128)(2,1)} %param.8) | copy-start | bytes 1572868
  148.8 38.3 %collective-permute-start.17 = (bf16[256,1792]{1,0:T(8,128)(2,1)S(1)}, bf16[256,1792]{1,0:T(8,128)(2,1)}, u32[]{:S(2)}, u32[]{:S(2)}) collective-permute-start(bf16[256,1792]{1,0:T(8,128)(2,1)S(1)} %bitcast.55), channel_id=1, source_target_pairs={{0,16},{16,0},{32,48},{48,32},{64,80},{80,64},{96,112},{112,96},{1... | collective-permute-start | bytes 2752520 | tf_op jit(solution)/shard_map/ppermute | solution.py:103
  150.8 35.5 %collective-permute-start.16 = (bf16[256,512]{1,0:T(8,128)(2,1)S(1)}, bf16[256,512]{1,0:T(8,128)(2,1)S(1)}, u32[]{:S(2)}, u32[]{:S(2)}) collective-permute-start(bf16[256,512]{1,0:T(8,128)(2,1)S(1)} %constant_dynamic-slice_fusion), channel_id=1, source_target_pairs={{0,0},{1,47},{2,78},{3,109},{4,140},{5,171},{6,202},{7,233},{8,264... | collective-permute-start | bytes 786440 | tf_op jit(solution)/shard_map/ppermute | solution.py:79
